TPU v7x, 32 devices: a whole 2x2x4 slice. The times are simulated.
32 devices in a mesh: row: 4 (over y, core), col: 8 (over z, x).
Axes of the slice: x: 2, y: 2, z: 4, core: 2. Of those that a mesh axis runs over, the one named last changes fastest.
Arguments:
- singles: bfloat16 [96, 384], P(('row', 'col')), may hold values from -6 to 6
- pair: float32 [96, 96, 128], P('row', 'col'), may hold values from -48 to 48
- frames: float32 [96, 12], P(('row', 'col')), may hold values from -9 to 9, as said below
- w_query: bfloat16 [384, 336], replicated, may hold values from -0.3125 to 0.3125
- w_keyval: bfloat16 [384, 816], replicated, may hold values from -0.3125 to 0.3125
- w_bias: float32 [128, 12], replicated, may hold values from -1 to 1
- head_weights: float32 [12], replicated, may hold values from -2 to 1
- w_out: bfloat16 [2112, 384], replicated, may hold values from -0.125 to 0.125
Outputs:
- update: float32 [96, 384], P(('row', 'col'))
Inputs may be any that keep to these rules, and one draw needn't show every extreme that they name: `frames`: the first nine entries of a row are a rotation matrix in row-major order, the last three a translation.
All inputs are finite; a program needn't handle non-finite values.
Results may differ from a plain program's by a relative error of at most 0.0029.
Values sent between devices are 32-bit elements; how exact they have to be, the bound alone decides.
A program may use at most 64 MiB of HBM per device.

v0:
```python
import math
import jax
import jax.numpy as jnp
from jax import lax
from jax.sharding import PartitionSpec as P

CS = 384
CZ = 128
H = 12
CH = 16
PQ = 4
PV = 8
HIGHEST = lax.Precision.HIGHEST


def broadcast(value, axis, source):
    kept = jnp.where(lax.axis_index(axis) == source, value, 0).astype(value.dtype)
    return lax.psum(kept, axis)


def rigid_apply(frames, points):
    rotation = frames[:, :9].reshape(frames.shape[0], 3, 3)
    moved = jnp.einsum("nab,nbm->nam", rotation, points, precision=HIGHEST)
    return moved + frames[:, 9:12, None]


def query_side(singles, frames, w_query):
    row_count = singles.shape[0]
    scalar_width = H * CH
    projected = jnp.dot(singles, w_query, preferred_element_type=jnp.float32)
    points = rigid_apply(frames, projected[:, scalar_width:].reshape(row_count, 3, H * PQ))
    return jnp.concatenate([projected[:, :scalar_width], points.reshape(row_count, 3 * H * PQ)], 1)


def key_side(singles, frames, w_keyval):
    row_count = singles.shape[0]
    scalar_width = 2 * H * CH
    point_end = scalar_width + 3 * H * PQ
    projected = jnp.dot(singles, w_keyval, preferred_element_type=jnp.float32)
    key_points = rigid_apply(
        frames, projected[:, scalar_width:point_end].reshape(row_count, 3, H * PQ)
    )
    value_points = rigid_apply(frames, projected[:, point_end:].reshape(row_count, 3, H * PV))
    return jnp.concatenate(
        [
            projected[:, :scalar_width],
            key_points.reshape(row_count, 3 * H * PQ),
            value_points.reshape(row_count, 3 * H * PV),
        ],
        1,
    )


def logits_of(query_feat, key_feat, pair_block, w_bias, head_weights):
    query_rows = query_feat.shape[0]
    key_rows = key_feat.shape[0]
    scalar_width = H * CH
    query_vec = query_feat[:, :scalar_width].reshape(query_rows, H, CH)
    query_points = query_feat[:, scalar_width:].reshape(query_rows, 3, H, PQ)
    key_vec = key_feat[:, :scalar_width].reshape(key_rows, H, CH)
    key_points = key_feat[:, 2 * scalar_width : 2 * scalar_width + 3 * H * PQ].reshape(
        key_rows, 3, H, PQ
    )
    scalar = jnp.einsum("ihc,jhc->ihj", query_vec, key_vec, precision=HIGHEST) / math.sqrt(CH)
    pair_bias = jnp.einsum("ijc,ch->ihj", pair_block, w_bias, precision=HIGHEST)
    cross_term = jnp.einsum("iahp,jahp->ihj", query_points, key_points, precision=HIGHEST)
    query_square = jnp.sum(query_points * query_points, axis=(1, 3))
    key_square = jnp.sum(key_points * key_points, axis=(1, 3))
    distance = query_square[:, :, None] + key_square.T[None, :, :] - 2.0 * cross_term
    weight = jax.nn.softplus(head_weights) * (math.sqrt(2.0 / (9.0 * PQ)) / 2.0)
    return math.sqrt(1.0 / 3.0) * (scalar + pair_bias - weight[None, :, None] * distance)


def weighted(exponent, key_feat, pair_block):
    key_rows = key_feat.shape[0]
    scalar_width = H * CH
    value_vec = key_feat[:, scalar_width : 2 * scalar_width].reshape(key_rows, H, CH)
    value_points = key_feat[:, 2 * scalar_width + 3 * H * PQ :].reshape(key_rows, 3, H, PV)
    weight_sum = jnp.sum(exponent, axis=2)
    scalar = jnp.einsum("ihj,jhc->ihc", exponent, value_vec, precision=HIGHEST)
    points = jnp.einsum("ihj,jahp->iahp", exponent, value_points, precision=HIGHEST)
    paired = jnp.einsum("ihj,ijc->ihc", exponent, pair_block, precision=HIGHEST)
    return (weight_sum, scalar, points, paired)


def finish_rest(scalar, points, frames, w_out):
    row_count = scalar.shape[0]
    rotation = frames[:, :9].reshape(row_count, 3, 3)
    relative = points - frames[:, 9:12, None, None]
    local_points = jnp.einsum("nba,nbhp->nahp", rotation, relative, precision=HIGHEST)
    length = jnp.sqrt(jnp.sum(local_points * local_points, axis=1) + 1.0)
    features = jnp.concatenate(
        [
            scalar.reshape(row_count, H * CH),
            local_points.reshape(row_count, 3 * H * PV),
            length.reshape(row_count, H * PV),
        ],
        1,
    )
    features = features.astype(jnp.bfloat16)
    return jnp.dot(features, w_out[: H * (CH + 4 * PV)], preferred_element_type=jnp.float32)


def paired_term(paired, w_out):
    row_count = paired.shape[0]
    pair_rows = w_out[H * (CH + 4 * PV) :].astype(jnp.float32)
    return jnp.dot(paired.reshape(row_count, H * CZ), pair_rows, precision=HIGHEST)


def finish(weight_sum, scalar, points, paired, frames, w_out):
    scalar = scalar / weight_sum[:, :, None]
    points = points / weight_sum[:, None, :, None]
    paired = paired / weight_sum[:, :, None]
    return finish_rest(scalar, points, frames, w_out) + paired_term(paired, w_out)


def block_size(total):
    chosen_size = 1
    for candidate in range(1, min(total, 32) + 1):
        if total % candidate == 0:
            chosen_size = candidate
    return chosen_size


def by_blocks(compute, arrays, total):
    size = block_size(total)
    count = total // size

    def one_block(start):
        pieces = [lax.dynamic_slice_in_dim(array, start, size, 0) for array in arrays]
        return compute(*pieces)

    starts = jnp.arange(count) * size
    results = lax.map(one_block, starts)
    return jax.tree.map(lambda value: value.reshape((total,) + value.shape[2:]), results)


def blocked_logits(query_feat, key_feat, pair, w_bias, head_weights):

    def compute(query_part, pair_part):
        return logits_of(query_part, key_feat, pair_part, w_bias, head_weights)

    return by_blocks(compute, [query_feat, pair], pair.shape[0])


def blocked_weighted(logits, shift, key_feat, pair):

    def compute(logit_part, shift_part, pair_part):
        return weighted(jnp.exp(logit_part - shift_part[:, :, None]), key_feat, pair_part)

    return by_blocks(compute, [logits, shift, pair], pair.shape[0])


def body(singles, pair, frames, w_query, w_keyval, w_bias, head_weights, w_out):
    rows_dev = singles.shape[0]
    query_rows = pair.shape[0]
    key_rows = pair.shape[1]
    column = lax.axis_index("col")
    ratio = query_rows // key_rows
    source = column // ratio
    within = column % ratio * key_rows
    packed = jnp.concatenate([singles.astype(jnp.float32), frames], 1)
    row_packed = lax.all_gather(packed, "col", axis=0, tiled=True)
    chosen = lax.dynamic_slice_in_dim(row_packed, within, key_rows, 0)
    arrived = broadcast(chosen, "row", source)
    query_feat = query_side(row_packed[:, :CS].astype(jnp.bfloat16), row_packed[:, CS:], w_query)
    key_feat = key_side(arrived[:, :CS].astype(jnp.bfloat16), arrived[:, CS:], w_keyval)
    logits = blocked_logits(query_feat, key_feat, pair, w_bias, head_weights)
    local_peak = jnp.max(logits, axis=2)
    own_start = column * rows_dev
    peak = lax.pmax(local_peak, "col")
    part_sum, part_scalar, part_points, part_paired = blocked_weighted(logits, peak, key_feat, pair)
    summed = lax.psum((part_sum, part_scalar, part_points, part_paired), "col")
    weight_sum, scalar, points, paired = [
        lax.dynamic_slice_in_dim(piece, own_start, rows_dev, 0) for piece in summed
    ]
    return finish(weight_sum, scalar, points, paired, frames, w_out)


def solution(mesh):
    return jax.shard_map(
        body,
        mesh=mesh,
        in_specs=(
            P(("row", "col"), None),
            P("row", "col", None),
            P(("row", "col"), None),
            P(),
            P(),
            P(),
            P(),
            P(),
        ),
        out_specs=P(("row", "col"), None),
        check_vma=False,
    )
```

profile of v0, /device:TPU:0, one launch (start us, length us, event | category | flops | bytes accessed | tf_op | source)
XLA Modules:
  0.0 156.1 jit_solution(14814837688478335846)
XLA Ops:
  6.6 0.7 convert_element_type.4
  7.3 0.7 maximum_bitcast_fusion
  8.0 32.3 %all-gather = f32[8,3,396]{2,1,0:T(4,128)S(1)} all-gather(f32[1,3,396]{2,1,0:T(4,128)S(1)} %maximum_bitcast_fusion), channel_id=1, replica_groups=mesh['row'=4,'col'=8] {'col'}, dimensions={0}, use_global_device_ids=true | all-gather | bytes 42768 | tf_op jit(solution)/shard_map/all_gather | solution.py:163
  40.5 10.3 %psum.35 = f32[12,396]{1,0:T(8,128)S(1)} all-reduce(f32[12,396]{1,0:T(8,128)S(1)} %dynamic-slice_select_fusion), channel_id=1, replica_groups=mesh['row'=4,'col'=8] {'row'}, use_global_device_ids=true, to_apply=%region_0.1 | all-reduce | flops 4752 | bytes 38016 | tf_op jit(solution)/shard_map/psum | solution.py:18
  50.9 1.1 fusion.22
  52.1 0.3 fusion.23
  52.6 0.2 multiply_reduce_fusion.2
  53.2 0.3 multiply_reduce_fusion.1
  54.1 0.8 fusion.24
  54.9 0.4 fusion.9
  55.3 0.3 fusion.37
  55.6 21.6 %pmax.7 = f32[24,12]{0,1:T(8,128)S(1)} all-reduce(f32[24,12]{0,1:T(8,128)S(1)} %get-tuple-element.60), channel_id=1, replica_groups=mesh['row'=4,'col'=8] {'col'}, use_global_device_ids=true, to_apply=%region_6.7 | all-reduce | flops 288 | bytes 2304 | tf_op jit(solution)/shard_map/pmax | solution.py:171
  77.2 0.2 copy.68
  77.4 1.0 fusion.15
  78.6 0.2 convolution_add_fusion.1
  79.0 0.4 convolution_bitcast_fusion
  79.5 0.2 convolution_bitcast_fusion.1
  79.8 36.4 %all-reduce = (f32[24,3,12,8]{0,3,1,2:T(8,128)S(1)}, f32[24,12]{0,1:T(8,128)S(1)}, f32[24,12,16]{0,2,1:T(8,128)S(1)}) all-reduce(f32[24,3,12,8]{0,3,1,2:T(8,128)S(1)} %convolution_bitcast_fusion, f32[24,12]{0,1:T(8,128)S(1)} %get-tuple-element.40, ...), channel_id=1, replica_groups=mesh['row'=4,'col'=8] {'col'}, use_global_device_ids=true, to_apply=%region_10.11 | all-reduce | flops 11808 | bytes 94464 | tf_op jit(solution)/shard_map/psum | solution.py:173
  116.5 0.3 copy.63
  116.9 0.3 convert_bitcast_fusion
  117.9 0.2 fusion.13
  118.1 29.1 %all-reduce.3.cloned.1.call-done = f32[24,12,128]{2,1,0:T(8,128)} async-done(((f32[24,12,128]{2,1,0:T(8,128)}), f32[24,12,128]{2,1,0:T(8,128)}) %all-reduce.3.cloned.1.call-update) | async-done | bytes 147472 | tf_op jit(solution)/shard_map/psum | solution.py:173
  147.2 0.8 divide_bitcast_fusion
  148.1 1.2 fusion.10
  (55 shorter events, 3.0 us)
Async XLA Ops:
  6.5 45.6 %copy-start = (bf16[384,816]{0,1:T(8,128)(2,1)S(1)}, bf16[384,816]{0,1:T(8,128)(2,1)}, u32[]{:S(2)}) copy-start(bf16[384,816]{0,1:T(8,128)(2,1)} %param.12) | copy-start | bytes 1880068
  6.5 47.3 %copy-start.5 = (f32[12]{0:T(128)S(1)}, f32[12]{0:T(128)}, u32[]{:S(2)}) copy-start(f32[12]{0:T(128)} %param.14) | copy-start | bytes 148
  6.5 47.5 %copy-start.2 = (f32[24,12,128]{2,0,1:T(8,128)S(1)}, f32[24,12,128]{2,0,1:T(8,128)}, u32[]{:S(2)}) copy-start(f32[24,12,128]{2,0,1:T(8,128)} %param.9) | copy-start | bytes 442372
  6.5 47.5 %copy-start.4 = (f32[128,12]{0,1:T(8,128)S(1)}, f32[128,12]{0,1:T(8,128)}, u32[]{:S(2)}) copy-start(f32[128,12]{0,1:T(8,128)} %param.13) | copy-start | bytes 18436
  6.5 140.7 %all-reduce.3.cloned.1.call-start = ((), (), s32[]{:S(2)}) async-start(), calls=%async_computation | async-start | bytes 393216 | tf_op jit(solution)/shard_map/psum | solution.py:173
  53.0 25.5 %copy-start.3 = (f32[3,12]{1,0:T(4,128)S(1)}, f32[3,12]{1,0:T(4,128)}, u32[]{:S(2)}) copy-start(f32[3,12]{1,0:T(4,128)} %param.10) | copy-start | bytes 436
  77.4 40.5 %copy-start.1 = (bf16[2112,384]{1,0:T(8,128)(2,1)S(1)}, bf16[2112,384]{1,0:T(8,128)(2,1)}, u32[]{:S(2)}) copy-start(bf16[2112,384]{1,0:T(8,128)(2,1)} %param.15) | copy-start | bytes 4866052
Sparse Core Ops, SparseCore 0:
  78.5 68.6 all-reduce.2
where the time goes:
time: 156 us
  blocking collectives  101 us (65%)
  waiting for transfers between devices  29.1 us (19%)
  between operations  13.7 us (9%)
  matrix products  6.99 us (4%)
  local copies, waits for them, and re-layouts  3.08 us (2%)
  other arithmetic  2.58 us (2%)
    psum x1, blocking collectives, body(): summed = lax.psum((part_sum, part_scalar, part_points, part_paired), 'col')  36.4 us
    all_gather x1, blocking collectives, body(): row_packed = lax.all_gather(packed, 'col', axis=0, tiled=True)  32.3 us
    psum x1, waiting for transfers between devices, body(): summed = lax.psum((part_sum, part_scalar, part_points, part_paired), 'col')  29.1 us
    pmax x1, blocking collectives, body(): peak = lax.pmax(local_peak, 'col')  21.6 us
    psum x1, blocking collectives, broadcast(): return lax.psum(kept, axis)  10.3 us
  transfers between devices with their start and end apart: 1, of which 1 were waited for; matrix products, arithmetic and copies ran while one was open for 2% of the time, Pallas kernels for 0%

commit v1 on v0

--- a/solution.py
+++ b/solution.py
@@ -15,7 +15,7 @@
 
 def broadcast(value, axis, source):
     kept = jnp.where(lax.axis_index(axis) == source, value, 0).astype(value.dtype)
-    return lax.psum(kept, axis)
+    return jnp.sum(lax.all_gather(kept, axis), axis=0)
 
 
 def rigid_apply(frames, points):

time: 156 us -> 151 us (0.968)
  blocking collectives: 101 us -> 95.4 us
    psum x1 -> x0, blocking collectives: 10.3 us -> none  [broadcast(): return lax.psum(kept, axis)]
    all_gather x0 -> x1, blocking collectives: none -> 5.42 us  [broadcast(): return jnp.sum(lax.all_gather(kept, axis), axis=0)]
where the time goes in v1:
time: 151 us
  blocking collectives  95.4 us (63%)
  waiting for transfers between devices  29 us (19%)
  between operations  13.7 us (9%)
  matrix products  6.99 us (5%)
  local copies, waits for them, and re-layouts  3.07 us (2%)
  other arithmetic  2.59 us (2%)
    psum x1, blocking collectives, body(): summed = lax.psum((part_sum, part_scalar, part_points, part_paired), 'col')  36.1 us
    all_gather x1, blocking collectives, body(): row_packed = lax.all_gather(packed, 'col', axis=0, tiled=True)  32.3 us
    psum x1, waiting for transfers between devices, body(): summed = lax.psum((part_sum, part_scalar, part_points, part_paired), 'col')  29 us
    pmax x1, blocking collectives, body(): peak = lax.pmax(local_peak, 'col')  21.6 us
    all_gather x1, blocking collectives, broadcast(): return jnp.sum(lax.all_gather(kept, axis), axis=0)  5.42 us
  transfers between devices with their start and end apart: 1, of which 1 were waited for; matrix products, arithmetic and copies ran while one was open for 2% of the time, Pallas kernels for 0%

profile of v1, /device:TPU:0, one launch (start us, length us, event | category | flops | bytes accessed | tf_op | source)
XLA Modules:
  0.0 150.8 jit_solution(12357624864383781855)
XLA Ops:
  6.6 0.7 convert_element_type.4
  7.3 0.7 maximum_bitcast_fusion
  8.0 32.3 %all-gather.1 = f32[8,3,396]{2,1,0:T(4,128)S(1)} all-gather(f32[1,3,396]{2,1,0:T(4,128)S(1)} %maximum_bitcast_fusion), channel_id=1, replica_groups=mesh['row'=4,'col'=8] {'col'}, dimensions={0}, use_global_device_ids=true | all-gather | bytes 42768 | tf_op jit(solution)/shard_map/all_gather | solution.py:163
  40.5 5.4 %all-gather.2 = f32[4,12,396]{2,1,0:T(8,128)S(1)} all-gather(f32[1,12,396]{2,1,0:T(8,128)S(1)} %select_bitcast_fusion), channel_id=2, replica_groups=mesh['row'=4,'col'=8] {'row'}, dimensions={0}, use_global_device_ids=true | all-gather | bytes 95040 | tf_op jit(solution)/shard_map/all_gather | solution.py:18
  46.0 1.1 fusion.22
  47.3 0.3 fusion.23
  47.8 0.2 multiply_reduce_fusion.2
  48.3 0.3 multiply_reduce_fusion.1
  49.2 0.8 fusion.24
  50.1 0.4 fusion.9
  50.5 0.3 fusion.37
  50.7 21.6 %pmax.7 = f32[24,12]{0,1:T(8,128)S(1)} all-reduce(f32[24,12]{0,1:T(8,128)S(1)} %get-tuple-element.60), channel_id=1, replica_groups=mesh['row'=4,'col'=8] {'col'}, use_global_device_ids=true, to_apply=%region_6.7 | all-reduce | flops 288 | bytes 2304 | tf_op jit(solution)/shard_map/pmax | solution.py:171
  72.3 0.2 copy.68
  72.5 1.0 fusion.15
  73.8 0.2 convolution_add_fusion.1
  74.2 0.4 convolution_bitcast_fusion
  74.6 0.2 convolution_bitcast_fusion.1
  75.0 36.1 %all-reduce = (f32[24,3,12,8]{0,3,1,2:T(8,128)S(1)}, f32[24,12]{0,1:T(8,128)S(1)}, f32[24,12,16]{0,2,1:T(8,128)S(1)}) all-reduce(f32[24,3,12,8]{0,3,1,2:T(8,128)S(1)} %convolution_bitcast_fusion, f32[24,12]{0,1:T(8,128)S(1)} %get-tuple-element.40, ...), channel_id=1, replica_groups=mesh['row'=4,'col'=8] {'col'}, use_global_device_ids=true, to_apply=%region_10.11 | all-reduce | flops 11808 | bytes 94464 | tf_op jit(solution)/shard_map/psum | solution.py:173
  111.4 0.3 copy.63
  111.8 0.3 convert_bitcast_fusion
  112.8 0.2 fusion.13
  113.0 29.0 %all-reduce.3.cloned.1.call-done = f32[24,12,128]{2,1,0:T(8,128)} async-done(((f32[24,12,128]{2,1,0:T(8,128)}), f32[24,12,128]{2,1,0:T(8,128)}) %all-reduce.3.cloned.1.call-update) | async-done | bytes 147472 | tf_op jit(solution)/shard_map/psum | solution.py:173
  142.0 0.8 divide_bitcast_fusion
  142.8 1.2 fusion.10
  (56 shorter events, 3.0 us)
Async XLA Ops:
  6.5 40.7 %copy-start = (bf16[384,816]{0,1:T(8,128)(2,1)S(1)}, bf16[384,816]{0,1:T(8,128)(2,1)}, u32[]{:S(2)}) copy-start(bf16[384,816]{0,1:T(8,128)(2,1)} %param.12) | copy-start | bytes 1880068
  6.5 42.5 %copy-start.5 = (f32[12]{0:T(128)S(1)}, f32[12]{0:T(128)}, u32[]{:S(2)}) copy-start(f32[12]{0:T(128)} %param.14) | copy-start | bytes 148
  6.5 42.7 %copy-start.2 = (f32[24,12,128]{2,0,1:T(8,128)S(1)}, f32[24,12,128]{2,0,1:T(8,128)}, u32[]{:S(2)}) copy-start(f32[24,12,128]{2,0,1:T(8,128)} %param.9) | copy-start | bytes 442372
  6.5 42.7 %copy-start.4 = (f32[128,12]{0,1:T(8,128)S(1)}, f32[128,12]{0,1:T(8,128)}, u32[]{:S(2)}) copy-start(f32[128,12]{0,1:T(8,128)} %param.13) | copy-start | bytes 18436
  6.5 135.4 %all-reduce.3.cloned.1.call-start = ((), (), s32[]{:S(2)}) async-start(), calls=%async_computation | async-start | bytes 393216 | tf_op jit(solution)/shard_map/psum | solution.py:173
  48.2 25.5 %copy-start.3 = (f32[3,12]{1,0:T(4,128)S(1)}, f32[3,12]{1,0:T(4,128)}, u32[]{:S(2)}) copy-start(f32[3,12]{1,0:T(4,128)} %param.10) | copy-start | bytes 436
  72.5 40.2 %copy-start.1 = (bf16[2112,384]{1,0:T(8,128)(2,1)S(1)}, bf16[2112,384]{1,0:T(8,128)(2,1)}, u32[]{:S(2)}) copy-start(bf16[2112,384]{1,0:T(8,128)(2,1)} %param.15) | copy-start | bytes 4866052
Sparse Core Ops, SparseCore 0:
  73.7 68.2 all-reduce.2
